TPU v7x, 128 devices: a whole 4x4x4 slice. The times are simulated.
128 devices in a mesh: left: 16 (over y, x_lo, core), right: 8 (over z, x_hi).
Axes of the slice: x: 4 (x_hi: 2, x_lo: 2; x = x_hi * 2 + x_lo), y: 4, z: 4, core: 2. Of those that a mesh axis runs over, the one named last changes fastest.
Arguments:
- tracer: float32 [2, 2048, 512, 256], P(None, None, 'left', 'right'), may hold values from -6 to 6
- symbol_x: float32 [2048], replicated, may hold values from 0.3 to 3
- symbol_y: float32 [512], replicated, may hold values from 0.3 to 3
- symbol_z: float32 [256], replicated, may hold values from 0.3 to 3
Outputs:
- modes: float32 [2, 2048, 512, 256], P(None, 'left', 'right')
All inputs are finite; a program needn't handle non-finite values.
Results may differ from a plain program's by a relative error of at most 0.00007.
Values sent between devices are 32-bit elements; how exact they have to be, the bound alone decides.
A program may use at most 256 MiB of HBM per device.

v0:
```python
import jax
import jax.numpy as jnp
from jax import lax
from jax.sharding import Mesh
from jax.sharding import PartitionSpec as P

LEFT = ("left_0", "left_1", "left_2")


def cut_along(shard, dim, count):
    before, after = (shard.shape[:dim], shard.shape[dim + 1 :])
    return jnp.moveaxis(shard.reshape(*before, count, -1, *after), dim, 0)


def laid_out(tiles, dim):
    tiles = jnp.moveaxis(tiles, 0, dim)
    lengths = tiles.shape
    return tiles.reshape(*lengths[:dim], lengths[dim] * lengths[dim + 1], *lengths[dim + 2 :])


def turned_blocks(tiles, axes, sequence):
    inside = tiles.shape[1:]
    filled = tiles.reshape(*(lax.axis_size(a) for a in axes), *inside)
    for k in sequence:
        filled = lax.all_to_all(filled, axes[k], k, k, tiled=True)
    return filled.reshape(-1, *inside)


def core_and_chips(shard, groups, sequence, split_dim, concat_dim):
    count = lax.axis_size(groups[0]) * lax.axis_size(groups[1])
    tiles = cut_along(shard, split_dim, count)
    return laid_out(turned_blocks(tiles, groups, sequence), concat_dim)


def transform_table(count):
    rank = jnp.arange(count)
    angle = 2.0 * jnp.pi / count * (rank[:, None] * rank[None, :] % count).astype(jnp.float32)
    return (jnp.cos(angle) + jnp.sin(angle)) * count ** (-0.5)


def transform_dim(values, dim):
    moved = jnp.tensordot(
        values,
        transform_table(values.shape[dim]),
        axes=([dim], [0]),
        precision=lax.Precision.HIGHEST,
    )
    return jnp.moveaxis(moved, -1, dim)


def local(tracer, symbol_x, symbol_y, symbol_z):

    def line_step(part_values):
        part_values = transform_dim(part_values, 1)
        part_values = core_and_chips(part_values, (("left_0", "left_1"), "left_2"), (0, 1), 1, 2)
        part_values = transform_dim(part_values, 2)
        return part_values

    middle_cut = tracer.shape[0] // 2
    lower_part = line_step(lax.slice_in_dim(tracer, 0, middle_cut, axis=0))
    upper_part = line_step(lax.slice_in_dim(tracer, middle_cut, tracer.shape[0], axis=0))
    pencil_values = jnp.concatenate([lower_part, upper_part], axis=0)
    pencil_values = lax.all_to_all(pencil_values, "right", split_axis=2, concat_axis=3, tiled=True)
    pencil_values = transform_dim(pencil_values, 3)
    share_x = pencil_values.shape[1]
    part_x = lax.dynamic_slice_in_dim(symbol_x, lax.axis_index(LEFT) * share_x, share_x)
    share_y = pencil_values.shape[2]
    part_y = lax.dynamic_slice_in_dim(symbol_y, lax.axis_index("right") * share_y, share_y)
    symbol = part_x[:, None, None] + part_y[None, :, None] + symbol_z[None, None, :]
    pencil_values = pencil_values * lax.rsqrt(symbol)
    return pencil_values


def solution(mesh):
    finer = Mesh(
        mesh.devices.reshape(4, 2, 2, mesh.shape["right"]), ("left_0", "left_1", "left_2", "right")
    )
    in_specs = (P(None, None, LEFT, "right"), P(), P(), P())
    out_specs = P(None, LEFT, "right", None)
    return jax.shard_map(local, mesh=finer, in_specs=in_specs, out_specs=out_specs, check_vma=False)
```

profile of v0, /device:TPU:0, one launch (start us, length us, event | category | flops | bytes accessed | tf_op | source)
XLA Modules:
  0.0 800.7 jit_solution(14855798524589440329)
XLA Ops:
  0.0 0.0 copy-start
  0.0 67.7 %add_multiply_fusion.9 = f32[2048,2048]{1,0:T(8,128)} fusion(), kind=kLoop, calls=%fused_computation.7.clone.1.clone | loop fusion | flops 67108864 | bytes 16777216
  67.7 0.0 copy-done
  67.7 6.3 fusion.70
  74.0 70.0 %fusion.11 = f32[2048,1024]{0,1} fusion(f32[2048,1024]{0,1:T(8,128)} %bitcast.74, f32[2048,2048]{1,0:T(8,128)} %add_multiply_fusion.9), kind=kOutput, calls=%fused_computation.18 | convolution fusion | flops 51539607552 | bytes 33554432
  144.0 11.7 %reshape_transpose_reshape.6 = f32[8,2,1,128,32,32]{3,1,0,5,4,2:T(2,128)} reshape(f32[1,2048,32,32]{1,3,2,0:T(8,128)} %bitcast.71) | data formatting | bytes 16777216 | tf_op jit(solution)/shard_map/reshape;transpose;reshape | solution.py:23
  155.7 7.5 copy.17
  163.2 5.5 all-to-all-start
  168.7 66.8 %add_multiply_fusion.8 = f32[2048,2048]{1,0:T(8,128)S(1)} fusion(), kind=kLoop, calls=%fused_computation.7.clone.clone.1 | loop fusion | flops 67108864 | bytes 16777216
  235.6 62.7 %fusion.10 = f32[2048,1024]{0,1} fusion(f32[2048,1024]{0,1:T(8,128)} %bitcast.73, f32[2048,2048]{1,0:T(8,128)S(1)} %add_multiply_fusion.8), kind=kOutput, calls=%fused_computation.17 | convolution fusion | flops 51539607552 | bytes 33554432
  298.3 11.8 %reshape_transpose_reshape.7 = f32[8,2,1,128,32,32]{3,1,0,5,4,2:T(2,128)} reshape(f32[1,2048,32,32]{1,3,2,0:T(8,128)} %bitcast.72) | data formatting | bytes 16777216 | tf_op jit(solution)/shard_map/reshape;transpose;reshape | solution.py:23
  310.1 7.4 copy.21
  317.5 0.0 all-to-all-done
  317.5 8.3 %copy.18 = f32[8,2,1,128,32,32]{3,0,5,4,2,1:T(8,128)S(1)} copy(f32[8,2,1,128,32,32]{3,1,5,4,2,0:T(2,128)} %all-to-all-done) | data formatting | bytes 16777216 | tf_op jit(solution)/shard_map/all_to_all | solution.py:25
  325.8 11.8 %all_to_all.38 = f32[8,2,1,128,32,32]{3,0,5,4,2,1:T(8,128)} all-to-all(f32[8,2,1,128,32,32]{3,0,5,4,2,1:T(8,128)S(1)} %copy.18), channel_id=1, replica_groups=mesh['left_0'=4,'left_1'=2,'left_2'=2,'right'=8] {'left_2'}, dimensions={1} | all-to-all | bytes 16777216 | tf_op jit(solution)/shard_map/all_to_all | solution.py:25
  337.6 5.7 all-to-all-start.2
  343.3 5.0 copy.19
  348.3 40.7 %fusion.12 = f32[1,128,512,32]{2,1,3,0:T(8,128)} fusion(f32[128,512,32]{0,2,1:T(8,128)S(1)} %bitcast.67), kind=kOutput, calls=%fused_computation.19 | convolution fusion | flops 12889096192 | bytes 16777216 | tf_op jit(solution)/shard_map/dot_general | solution.py:42
  389.0 49.1 %all-to-all-done.2 = f32[8,2,1,128,32,32]{3,1,5,4,2,0:T(2,128)} async-done(((f32[8,2,1,128,32,32]{3,1,5,4,2,0:T(2,128)}), f32[8,2,1,128,32,32]{3,1,5,4,2,0:T(2,128)}, u32[]{:S(2)}, u32[]{:S(2)}) %all-to-all-start.2) | async-done | bytes 8388640 | tf_op jit(solution)/shard_map/all_to_all | solution.py:25
  438.1 8.3 %copy.22 = f32[8,2,1,128,32,32]{3,0,5,4,2,1:T(8,128)S(1)} copy(f32[8,2,1,128,32,32]{3,1,5,4,2,0:T(2,128)} %all-to-all-done.2) | data formatting | bytes 16777216 | tf_op jit(solution)/shard_map/all_to_all | solution.py:25
  446.4 10.5 %all_to_all.39 = f32[8,2,1,128,32,32]{3,0,5,4,2,1:T(8,128)S(1)} all-to-all(f32[8,2,1,128,32,32]{3,0,5,4,2,1:T(8,128)S(1)} %copy.22), channel_id=1, replica_groups=mesh['left_0'=4,'left_1'=2,'left_2'=2,'right'=8] {'left_2'}, dimensions={1} | all-to-all | bytes 16777216 | tf_op jit(solution)/shard_map/all_to_all | solution.py:25
  456.9 0.0 slice-start
  456.9 1.6 copy.23
  458.5 0.0 slice-start.1
  458.5 51.9 %fusion.15 = f32[1,128,512,32]{2,1,3,0:T(8,128)} fusion(f32[128,512,32]{0,2,1:T(8,128)S(1)} %bitcast.68), kind=kOutput, calls=%fused_computation.20 | convolution fusion | flops 12889096192 | bytes 16777216 | tf_op jit(solution)/shard_map/dot_general | solution.py:42
  510.4 0.0 slice-done
  510.4 0.0 slice-done.1
  510.4 10.1 %pad_maximum_fusion = f32[2,128,512,32]{2,1,3,0:T(8,128)} fusion(f32[1,128,512,32]{2,1,3,0:T(8,128)} %fusion.15, f32[1,128,512,32]{2,1,3,0:T(8,128)S(1)} %bitcast.70), kind=kLoop, calls=%fused_computation.6 | loop fusion | flops 4194304 | bytes 33554432 | tf_op jit(solution)/shard_map/concatenate | solution.py:62
  520.5 19.9 %copy.25 = f32[2,128,512,32]{1,3,0,2:T(8,128)} copy(f32[2,128,512,32]{2,1,3,0:T(8,128)} %pad_maximum_fusion) | data formatting | bytes 33554432 | tf_op jit(solution)/shard_map/concatenate | solution.py:62
  540.4 0.0 copy-start.1
  540.4 7.6 all-to-all-start.4
  548.0 0.8 dynamic_slice.6
  548.7 0.8 dynamic_slice.7
  549.5 0.1 broadcast_add_fusion
  549.6 0.0 copy-done.1
  549.6 3.8 add_rsqrt_fusion
  553.4 180.8 %all-to-all-done.4 = f32[2,128,512,32]{1,3,0,2:T(8,128)} async-done(((f32[2,128,512,32]{1,3,0,2:T(8,128)}), f32[2,128,512,32]{1,3,0,2:T(8,128)}, u32[]{:S(2)}, u32[]{:S(2)}) %all-to-all-start.4) | async-done | bytes 16777248 | tf_op jit(solution)/shard_map/all_to_all | solution.py:63
  734.2 12.2 %copy.27 = f32[2,128,64,8,32]{1,4,3,2,0:T(8,128)} copy(f32[2,128,64,8,32]{1,4,0,2,3:T(8,128)} %bitcast.25) | data formatting | bytes 33554432 | tf_op jit(solution)/shard_map/all_to_all | solution.py:63
  746.4 36.3 %broadcast_multiply_fusion = f32[2,128,64,256]{3,1,2,0:T(8,128)} fusion(f32[128,64,256]{2,0,1:T(8,128)} %add_rsqrt_fusion, f32[2,128,64,256]{1,3,2,0:T(8,128)} %bitcast.66), kind=kOutput, calls=%fused_computation.15 | convolution fusion | flops 12890144768 | bytes 41943040 | tf_op jit(solution)/shard_map/dot_general | solution.py:42
  782.7 17.8 %copy.29 = f32[2,128,64,256]{3,2,1,0:T(8,128)} copy(f32[2,128,64,256]{3,1,2,0:T(8,128)} %broadcast_multiply_fusion) | data formatting | bytes 33554432 | tf_op jit(solution)/shard_map/mul | solution.py:70
  (1 shorter events, 0.0 us)
Async XLA Ops:
  0.0 67.7 %copy-start = (f32[2,2048,32,32]{1,3,2,0:T(8,128)S(1)}, f32[2,2048,32,32]{1,3,2,0:T(8,128)}, u32[]{:S(2)}) copy-start(f32[2,2048,32,32]{1,3,2,0:T(8,128)} %param.4) | copy-start | bytes 50331652
  163.2 154.3 %all-to-all-start = ((f32[8,2,1,128,32,32]{3,1,5,4,2,0:T(2,128)}), f32[8,2,1,128,32,32]{3,1,5,4,2,0:T(2,128)}, u32[]{:S(2)}, u32[]{:S(2)}) async-start(f32[8,2,1,128,32,32]{3,1,5,4,2,0:T(2,128)} %copy.17), calls=%async_computation | async-start | bytes 16777216 | tf_op jit(solution)/shard_map/all_to_all | solution.py:25
  337.6 100.5 %all-to-all-start.2 = ((f32[8,2,1,128,32,32]{3,1,5,4,2,0:T(2,128)}), f32[8,2,1,128,32,32]{3,1,5,4,2,0:T(2,128)}, u32[]{:S(2)}, u32[]{:S(2)}) async-start(f32[8,2,1,128,32,32]{3,1,5,4,2,0:T(2,128)} %copy.21), calls=%async_computation.2 | async-start | bytes 16777216 | tf_op jit(solution)/shard_map/all_to_all | solution.py:25
  456.9 53.5 %slice-start = ((s8[8388608]{0:T(1024)(128)(4,1)}), s8[4194304]{0:T(1024)(128)(4,1)S(1)}, s32[]{:S(2)}) async-start(s8[8388608]{0:T(1024)(128)(4,1)} %bitcast.69), calls=%async_computation.5 | async-start | bytes 8388608
  458.5 51.9 %slice-start.1 = ((s8[8388608]{0:T(1024)(128)(4,1)}), s8[4194304]{0:T(1024)(128)(4,1)S(1)}, s32[]{:S(2)}) async-start(s8[8388608]{0:T(1024)(128)(4,1)} %bitcast.69), calls=%async_computation.6 | async-start | bytes 8388608
  540.4 9.2 %copy-start.1 = (f32[256]{0:T(256)S(1)}, f32[256]{0:T(256)}, u32[]{:S(2)}) copy-start(f32[256]{0:T(256)} %param.7) | copy-start | bytes 3076
  540.4 193.8 %all-to-all-start.4 = ((f32[2,128,512,32]{1,3,0,2:T(8,128)}), f32[2,128,512,32]{1,3,0,2:T(8,128)}, u32[]{:S(2)}, u32[]{:S(2)}) async-start(f32[2,128,512,32]{1,3,0,2:T(8,128)} %copy.25), calls=%async_computation.4 | async-start | bytes 33554432 | tf_op jit(solution)/shard_map/all_to_all | solution.py:63
where the time goes:
time: 808 us; the launch traced here: 801 us
  matrix products  262 us (32%)
  waiting for transfers between devices  230 us (28%)
  other arithmetic  148 us (18%)
  local copies, waits for them, and re-layouts  119 us (15%)
  blocking collectives  22.3 us (3%)
  starting transfers between devices  18.8 us (2%)
    all_to_all x1, waiting for transfers between devices, local(): lax.all_to_all(pencil_values, 'right', split_axis=2, concat_axis=3, tiled...  181 us
    unnamed x3, other arithmetic  135 us
    unnamed x2, matrix products  133 us
    dot_general x3, matrix products, transform_dim(): jnp.tensordot(values, transform_table(values.shape[dim]), axes=([dim], [0...  129 us
    all_to_all x2, waiting for transfers between devices, turned_blocks(): filled = lax.all_to_all(filled, axes[k], k, k, tiled=True)  49.1 us
    another operation x4, local copies, waits for them, and re-layouts, turned_blocks(): filled = tiles.reshape(*(lax.axis_size(a) for a in axes), *inside)  38.4 us
    all_to_all x4, local copies, waits for them, and re-layouts, turned_blocks(): filled = lax.all_to_all(filled, axes[k], k, k, tiled=True)  23.2 us
    all_to_all x2, blocking collectives, turned_blocks(): filled = lax.all_to_all(filled, axes[k], k, k, tiled=True)  22.3 us
  transfers between devices with their start and end apart: 3, of which 2 were waited for; matrix products, arithmetic and copies ran while one was open for 25% of the time, Pallas kernels for 0%

commit v1 on v0

v1 whole, which is shorter than its diff:
```python
import functools

import jax
import jax.numpy as jnp
import numpy as np
from jax import lax
from jax.experimental import pallas as pl
from jax.experimental.pallas import tpu as pltpu
from jax.sharding import PartitionSpec as P

MESH = pl.DeviceIdType.MESH
RADIX = 16
PAIRS = 8
LANES = 128
CHUNKS = 8
VMEM_BYTES = 67043328


def partner(pair):
    return (0, 8) if pair == 0 else (pair, RADIX - pair)


def split_bf16(table):
    high = table.astype(jnp.bfloat16)
    low = (table - high.astype(np.float32)).astype(jnp.bfloat16)
    return np.asarray(high), np.asarray(low)


def pair_blocks(count):
    inner = count // RADIX
    blocks = np.zeros((PAIRS, 2, 2, inner, inner), np.float64)
    i = np.arange(inner)[:, None]
    q = np.arange(inner)[None, :]
    for pair in range(PAIRS):
        ids = partner(pair)
        for half in range(2):
            angle = 2 * np.pi * ((i * (ids[half] + RADIX * q)) % count) / count
            if pair == 0:
                blocks[pair, half, half] = np.cos(angle) + np.sin(angle)
            else:
                blocks[pair, half, half] = np.cos(angle)
                blocks[pair, half, 1 - half] = np.sin(angle)
    return blocks / np.sqrt(count)


def stacked_tables(table):
    high, low = split_bf16(table.astype(np.float32))
    return np.concatenate([high, low], axis=1)


def x_tables():
    blocks = pair_blocks(2048)
    q = blocks.reshape(PAIRS, 2, 2, 128, 16, 8)
    rows = np.transpose(q, (0, 4, 1, 5, 2, 3))
    return stacked_tables(rows.reshape(PAIRS, 256, 256))


def y_tables():
    blocks = pair_blocks(512)
    v = blocks.reshape(PAIRS, 2, 2, 32, 8, 4)
    full = np.einsum("pabrdv,jk->pdvjabrk", v, np.eye(4))
    return stacked_tables(full.reshape(PAIRS, 256, 256))


def z_table():
    src, zc, j = np.meshgrid(np.arange(8), np.arange(8), np.arange(4), indexing="ij")
    z = (32 * src + 8 * j + zc).reshape(-1)
    k = np.arange(256)
    angle = 2 * np.pi * ((z[:, None] * k[None, :]) % 256) / 256
    table = ((np.cos(angle) + np.sin(angle)) / 16.0).astype(np.float32)
    high, low = split_bf16(table)
    return np.stack([high, low])


def small_hartley(v):
    n = len(v)
    if n == 1:
        return v
    half = n // 2
    even = small_hartley(v[0::2])
    odd = small_hartley(v[1::2])
    out = [None] * n
    for k in range(half):
        c = float(np.cos(2 * np.pi * k / n))
        s = float(np.sin(2 * np.pi * k / n))
        back = odd[-k % half]
        if k == 0:
            turned = odd[0]
        elif 4 * k == n:
            turned = back
        elif 8 * k == n:
            turned = (odd[k] + back) * c
        elif 8 * k == 3 * n:
            turned = (back - odd[k]) * s
        else:
            turned = odd[k] * c + back * s
        out[k] = even[k] + turned
        out[k + half] = even[k] - turned
    return out


NT = (((1,), (1,)), ((), ()))
TN = (((0,), (0,)), ((), ()))


def radix_step(load, high_ref, low_ref):
    def rows(t, carry):
        zz, g = t // 8, t % 8
        parts = small_hartley(load(zz, g))
        at = pl.ds(pl.multiple_of(zz * 128 + g * 16, 16), 16)
        for pair in range(PAIRS):
            for half, p in enumerate(partner(pair)):
                value = parts[p]
                high = value.astype(jnp.bfloat16)
                low = (value - high.astype(jnp.float32)).astype(jnp.bfloat16)
                lanes = slice(half * LANES, (half + 1) * LANES)
                high_ref[pair, at, lanes] = high
                low_ref[pair, at, lanes] = low
        return carry

    lax.fori_loop(0, 16, rows, 0)


def matmul_step(table_ref, high_ref, low_ref, store):
    def one(pair, carry):
        high = high_ref[pair]
        table = table_ref[pair]
        both = lax.dot_general(table, high, NT, preferred_element_type=jnp.float32)
        rest = lax.dot_general(table[:256], low_ref[pair], NT, preferred_element_type=jnp.float32)
        store(pair, both[:256] + both[256:] + rest)
        return carry

    lax.fori_loop(0, PAIRS, one, 0)


def exchange_kernel(
    x_hbm, wx_hbm, wy_hbm, l_hbm, r_hbm,
    x_ref, wx_ref, wy_ref, xo_ref, lb_ref, yo_ref, high_ref, low_ref,
    load_sem, table_sem, fetch_sem,
    l_send, l_recv, l_own, r_send, r_recv, r_own,
):
    left = lax.axis_index("left")
    right = lax.axis_index("right")

    def left_peer(o):
        return (lax.rem(left + o, 16), right)

    def right_peer(o):
        return (left, lax.rem(right + o, 8))

    def x_load(f, a):
        lanes = pl.ds(pl.multiple_of(a * LANES, LANES), LANES)
        return pltpu.make_async_copy(x_hbm.at[f, :, lanes], x_ref.at[a], load_sem.at[a])

    def x_start(f):
        def one(a, carry):
            x_load(f, a).start()
            return carry

        lax.fori_loop(0, RADIX, one, 0)

    def x_wait(f):
        def one(a, carry):
            x_load(f, a).wait()
            return carry

        lax.fori_loop(0, RADIX, one, 0)

    def wx_load():
        return pltpu.make_async_copy(wx_hbm, wx_ref, table_sem.at[0])

    def wy_load():
        return pltpu.make_async_copy(wy_hbm, wy_ref, table_sem.at[1])

    x_start(0)
    wx_load().start()

    barrier = pltpu.get_barrier_semaphore()

    def greet_left(o, carry):
        pl.semaphore_signal(barrier, inc=1, device_id=left_peer(o), device_id_type=MESH)
        return carry

    def greet_right(o, carry):
        pl.semaphore_signal(barrier, inc=1, device_id=right_peer(o), device_id_type=MESH)
        return carry

    lax.fori_loop(1, 16, greet_left, 0)
    lax.fori_loop(1, 8, greet_right, 0)
    pl.semaphore_wait(barrier, 22)

    def l_copy(c, o):
        to = lax.rem(left + o, 16)
        return pltpu.make_async_remote_copy(
            src_ref=xo_ref.at[c, to],
            dst_ref=l_hbm.at[c, left],
            send_sem=l_send.at[c, o],
            recv_sem=l_recv.at[c, o],
            device_id=(to, right),
            device_id_type=MESH,
        )

    def l_keep(c):
        return pltpu.make_async_copy(xo_ref.at[c, left], l_hbm.at[c, left], l_own.at[c])

    def r_copy(c, o):
        to = lax.rem(right + o, 8)
        rows = pl.ds(pl.multiple_of((c % 4) * 16, 16), 16)
        return pltpu.make_async_remote_copy(
            src_ref=yo_ref.at[c, to],
            dst_ref=r_hbm.at[right, c // 4, :, rows],
            send_sem=r_send.at[c, o],
            recv_sem=r_recv.at[c, o],
            device_id=(left, to),
            device_id_type=MESH,
        )

    def r_keep(c):
        rows = pl.ds(pl.multiple_of((c % 4) * 16, 16), 16)
        return pltpu.make_async_copy(yo_ref.at[c, right], r_hbm.at[right, c // 4, :, rows], r_own.at[c])

    wx_load().wait()

    def x_chunk(c, carry):
        @pl.when(c == 0)
        def _():
            x_wait(0)
            wy_load().start()

        @pl.when(c == 4)
        def _():
            x_start(1)
            x_wait(1)

        first = (c % 4) * 2

        def load(zz, g):
            rows = pl.ds(g * 128 + first + zz, 16, stride=8)
            return [x_ref[a, rows, :] for a in range(RADIX)]

        def store(pair, value):
            at = pl.ds(pl.multiple_of(pair * 16, 16), 16)
            for zz in range(2):
                xo_ref[c, :, zz, at, :] = value[:, zz * LANES : (zz + 1) * LANES].reshape(16, 16, LANES)

        radix_step(load, high_ref, low_ref)
        matmul_step(wx_ref, high_ref, low_ref, store)

        def send(o, carry):
            l_copy(c, o).start()
            return carry

        lax.fori_loop(1, 16, send, 0)
        l_keep(c).start()
        return carry

    lax.fori_loop(0, CHUNKS, x_chunk, 0)
    wy_load().wait()

    def y_chunk(c, carry):
        def arrive(o, carry):
            l_copy(c, o).wait_recv()
            return carry

        l_keep(c).wait()
        lax.fori_loop(1, 16, arrive, 0)
        fetch = pltpu.make_async_copy(l_hbm.at[c], lb_ref, fetch_sem)
        fetch.start()
        fetch.wait()

        def load(zz, g):
            rows = pl.ds(pl.multiple_of(g * 16, 16), 16)
            return [lb_ref[s, zz, rows, :] for s in range(RADIX)]

        def store(pair, value):
            at = pl.ds(pl.multiple_of(pair * 4, 4), 4)
            for zz in range(2):
                yo_ref[c, :, at, zz * 8 : (zz + 1) * 8, :] = value[:, zz * LANES : (zz + 1) * LANES].reshape(
                    8, 4, 8, LANES
                )

        radix_step(load, high_ref, low_ref)
        matmul_step(wy_ref, high_ref, low_ref, store)

        def send(o, carry):
            r_copy(c, o).start()
            return carry

        lax.fori_loop(1, 8, send, 0)
        r_keep(c).start()
        return carry

    lax.fori_loop(0, CHUNKS, y_chunk, 0)

    def finish(c, carry):
        def l_done(o, carry):
            l_copy(c, o).wait_send()
            return carry

        def r_done(o, carry):
            r_copy(c, o).wait()
            return carry

        lax.fori_loop(1, 16, l_done, 0)
        lax.fori_loop(1, 8, r_done, 0)
        r_keep(c).wait()
        return carry

    lax.fori_loop(0, CHUNKS, finish, 0)


def exchange(x, wx, wy):
    f32 = jnp.float32
    dma = pltpu.SemaphoreType.DMA
    hbm = pl.BlockSpec(memory_space=pltpu.HBM)
    _, r = pl.pallas_call(
        exchange_kernel,
        out_shape=(
            jax.ShapeDtypeStruct((CHUNKS, 16, 2, 128, LANES), f32),
            jax.ShapeDtypeStruct((8, 2, 32, 64, LANES), f32),
        ),
        in_specs=[hbm] * 3,
        out_specs=(hbm, hbm),
        scratch_shapes=[
            pltpu.VMEM((RADIX, 1024, LANES), f32),
            pltpu.VMEM((PAIRS, 512, 256), jnp.bfloat16),
            pltpu.VMEM((PAIRS, 512, 256), jnp.bfloat16),
            pltpu.VMEM((CHUNKS, 16, 2, 128, LANES), f32),
            pltpu.VMEM((16, 2, 128, LANES), f32),
            pltpu.VMEM((CHUNKS, 8, 32, 16, LANES), f32),
            pltpu.VMEM((PAIRS, 256, 256), jnp.bfloat16),
            pltpu.VMEM((PAIRS, 256, 256), jnp.bfloat16),
            dma((RADIX,)),
            dma((2,)),
            dma,
            dma((CHUNKS, 16)),
            dma((CHUNKS, 16)),
            dma((CHUNKS,)),
            dma((CHUNKS, 8)),
            dma((CHUNKS, 8)),
            dma((CHUNKS,)),
        ],
        compiler_params=pltpu.CompilerParams(
            collective_id=0, has_side_effects=True, vmem_limit_bytes=VMEM_BYTES
        ),
        name="exchange",
    )(x, wx, wy)
    return r


def last_kernel(sy_ref, r_ref, h_ref, sx_ref, sz_ref, o_hbm, o_ref, high_ref, low_ref, base_ref, o_sem):
    step = pl.program_id(0)
    vlo = step % 4
    slot = step % 2

    def out_copy(at_step, lane):
        where = at_step % 2
        return pltpu.make_async_copy(
            o_ref.at[where, lane],
            o_hbm.at[at_step // 4, :, pl.ds(pl.multiple_of(at_step % 4 * 16, 16), 16), pl.ds(lane * LANES, LANES)],
            o_sem.at[where, lane],
        )

    base_ref[...] = sx_ref[...] + sz_ref[...]
    for pair in range(PAIRS):
        for half, u in enumerate(partner(pair)):
            rows = [r_ref[src, 0, pair, 0, pl.ds(half, 32, stride=2), :] for src in range(8)]
            value = jnp.concatenate(rows, axis=0)
            high = value.astype(jnp.bfloat16)
            low = (value - high.astype(jnp.float32)).astype(jnp.bfloat16)
            high_ref[:, u * LANES : (u + 1) * LANES] = high
            low_ref[:, u * LANES : (u + 1) * LANES] = low

    @pl.when(step >= 2)
    def _():
        for lane in range(2):
            out_copy(step - 2, lane).wait()

    def some(t, carry):
        at = pl.ds(pl.multiple_of(t * 512, 512), 512)
        high = high_ref[:, at]
        acc = lax.dot_general(high, h_ref[0], TN, preferred_element_type=jnp.float32)
        acc += lax.dot_general(high, h_ref[1], TN, preferred_element_type=jnp.float32)
        acc += lax.dot_general(low_ref[:, at], h_ref[0], TN, preferred_element_type=jnp.float32)
        for i in range(4):
            u = t * 4 + i
            scale = lax.rsqrt(base_ref[...] + sy_ref[vlo * 16 + u])
            value = acc[i * 128 : (i + 1) * 128] * scale
            for lane in range(2):
                flat = o_ref.at[slot, lane].reshape(2048, LANES)
                for pair in range(PAIRS):
                    for half, p in enumerate(partner(pair)):
                        at_row = pair * 16 + half * 8
                        flat[pl.ds(p * 16 + u, 8, stride=256), :] = value[
                            at_row : at_row + 8, lane * LANES : (lane + 1) * LANES
                        ]
        return carry

    lax.fori_loop(0, 4, some, 0)
    for lane in range(2):
        out_copy(step, lane).start()

    @pl.when(step == 7)
    def _():
        for lane in range(2):
            out_copy(step - 1, lane).wait()
            out_copy(step, lane).wait()


def last(r, h, sx, sy, sz):
    f32 = jnp.float32
    return pl.pallas_call(
        last_kernel,
        grid=(8,),
        out_shape=jax.ShapeDtypeStruct((2, 128, 64, 256), f32),
        in_specs=[
            pl.BlockSpec(memory_space=pltpu.SMEM),
            pl.BlockSpec((8, 1, 8, 1, 64, LANES), lambda i: (0, i // 4, 0, i % 4, 0, 0)),
            pl.BlockSpec((2, 256, 256), lambda i: (0, 0, 0)),
            pl.BlockSpec((128, 1), lambda i: (0, 0)),
            pl.BlockSpec((1, 256), lambda i: (0, 0)),
        ],
        out_specs=pl.BlockSpec(memory_space=pltpu.HBM),
        scratch_shapes=[
            pltpu.VMEM((2, 2, 128, 16, LANES), f32),
            pltpu.VMEM((256, 2048), jnp.bfloat16),
            pltpu.VMEM((256, 2048), jnp.bfloat16),
            pltpu.VMEM((128, 256), f32),
            pltpu.SemaphoreType.DMA((2, 2)),
        ],
        compiler_params=pltpu.CompilerParams(vmem_limit_bytes=VMEM_BYTES),
        name="last",
    )(sy, r.reshape(8, 2, 8, 4, 64, LANES), h, sx, sz)


def local(tracer, symbol_x, symbol_y, symbol_z):
    x = jnp.transpose(tracer, (0, 2, 3, 1)).reshape(2, 1024, 2048)
    r = exchange(x, x_tables(), y_tables())
    part_x = lax.dynamic_slice_in_dim(symbol_x, lax.axis_index("left") * 128, 128)
    part_y = lax.dynamic_slice_in_dim(symbol_y, lax.axis_index("right") * 64, 64)
    sx = part_x.reshape(8, 16).T[np.asarray([p for pair in range(PAIRS) for p in partner(pair)])].reshape(128, 1)
    return last(r, z_table(), sx, part_y, symbol_z.reshape(1, 256))


def solution(mesh):
    in_specs = (P(None, None, "left", "right"), P(), P(), P())
    out_specs = P(None, "left", "right", None)
    return jax.shard_map(local, mesh=mesh, in_specs=in_specs, out_specs=out_specs, check_vma=False)
```

time: 808 us -> 425 us (0.53)
  Pallas kernels: 0 us -> 419 us
  matrix products: 262 us -> 0 us
  waiting for transfers between devices: 230 us -> 0 us
  other arithmetic: 148 us -> 0.66 us
  local copies, waits for them, and re-layouts: 119 us -> 3.48 us
  blocking collectives: 22.3 us -> 0 us
  starting transfers between devices: 18.8 us -> 0 us
    pallas_call x0 -> x2, Pallas kernels: none -> 419 us  [the longest x1 383 us: exchange(): pl.pallas_call(exchange_kernel, out_shape=(jax.ShapeDtypeStruct((CHUNKS,...]
    all_to_all x3 -> x0, waiting for transfers between devices: 230 us -> none  [the longest x1 181 us: local(): lax.all_to_all(pencil_values, 'right', split_axis=2, concat_axis=3, tiled...]
    unnamed x3 -> x0, other arithmetic: 135 us -> none
    unnamed x2 -> x0, matrix products: 133 us -> none
    dot_general x3 -> x0, matrix products: 129 us -> none  [transform_dim(): jnp.tensordot(values, transform_table(values.shape[dim]), axes=([dim], [0...]
    another operation x4 -> x0, local copies, waits for them, and re-layouts: 38.4 us -> none  [turned_blocks(): filled = tiles.reshape(*(lax.axis_size(a) for a in axes), *inside)]
    all_to_all x5 -> x0, local copies, waits for them, and re-layouts: 35.4 us -> none  [the longest x4 23.2 us: turned_blocks(): filled = lax.all_to_all(filled, axes[k], k, k, tiled=True)]
    all_to_all x2 -> x0, blocking collectives: 22.3 us -> none  [turned_blocks(): filled = lax.all_to_all(filled, axes[k], k, k, tiled=True)]
  transfers between devices with their start and end apart: 3 -> 0, of which waited for: 2 -> 0; matrix products, arithmetic and copies ran while one was open for 25% -> 0% of each run, Pallas kernels for 0% -> 0%
where the time goes in v1:
time: 425 us; the launch traced here: 423 us
  Pallas kernels  419 us (99%)
    pallas_call x1, Pallas kernels, exchange(): pl.pallas_call(exchange_kernel, out_shape=(jax.ShapeDtypeStruct((CHUNKS,...  383 us
    pallas_call x1, Pallas kernels, last(): pl.pallas_call(last_kernel, grid=(8,), out_shape=jax.ShapeDtypeStruct((2,...  35.2 us

profile of v1, /device:TPU:0, one launch (start us, length us, event | category | flops | bytes accessed | tf_op | source)
XLA Modules:
  0.0 422.8 jit_solution(1873029808499525238)
XLA Ops:
  0.0 1.3 dynamic_slice.6.sy_ref
  1.3 383.4 %exchange.1 = (f32[8,16,2,128,128]{4,3,2,1,0:T(8,128)}, f32[8,2,32,64,128]{4,3,2,1,0:T(8,128)}) custom-call(f32[2,1024,2048]{2,1,0:T(8,128)} %bitcast.6, bf16[8,512,256]{2,1,0:T(8,128)(2,1)} %constant.31.clone.wx_hbm, bf16[8,512,256]{2,1,0:T(8,128)(2,1)} %constant.32.clone.wy_hbm), custom_call_target="tpu_custom_call" | custom-call | tf_op jit(solution)/shard_map/exchange/pallas_call | solution.py:316
  384.8 0.8 dynamic_slice.7
  385.5 0.1 reshape.17
  385.6 0.1 copy.12
  385.7 0.7 pad_clamp_fusion
  386.3 0.6 gather_fusion
  386.9 0.7 reshape.28.sx_ref
  387.6 35.2 %last.1 = f32[2,128,64,256]{3,2,1,0:T(8,128)} custom-call(f32[64]{0:T(128)} %dynamic_slice.6.sy_ref, f32[8,2,8,4,64,128]{5,4,3,2,1,0:T(8,128)} %bitcast.7, bf16[2,256,256]{2,1,0:T(8,128)(2,1)} %constant.35.clone.h_ref, f32[128,1]{1,0:T(8,128)} %reshape.28.sx_ref, f32[1,256]{1,0:T(1,128)} %bitcast.9), custom_call_target="tpu_custom_call" | custom-call | tf_op jit(solution)/shard_map/last/pallas_call | solution.py:412

commit v2 on v1

v2 whole, which is shorter than its diff:
```python
import jax
import jax.numpy as jnp
import numpy as np
from jax import lax
from jax.experimental import pallas as pl
from jax.experimental.pallas import tpu as pltpu
from jax.sharding import PartitionSpec as P

MESH = pl.DeviceIdType.MESH
RADIX = 16
PAIRS = 8
LANES = 128
CHUNKS = 8
VMEM_BYTES = 46 * 2**20
PITCH = 136
UNROLL = 2


def partner(pair):
    return (0, 8) if pair == 0 else (pair, RADIX - pair)


def split_bf16(table):
    high = table.astype(jnp.bfloat16)
    low = (table - high.astype(np.float32)).astype(jnp.bfloat16)
    return np.asarray(high), np.asarray(low)


def pair_blocks(count):
    inner = count // RADIX
    blocks = np.zeros((PAIRS, 2, 2, inner, inner), np.float64)
    i = np.arange(inner)[:, None]
    q = np.arange(inner)[None, :]
    for pair in range(PAIRS):
        ids = partner(pair)
        for half in range(2):
            angle = 2 * np.pi * ((i * (ids[half] + RADIX * q)) % count) / count
            if pair == 0:
                blocks[pair, half, half] = np.cos(angle) + np.sin(angle)
            else:
                blocks[pair, half, half] = np.cos(angle)
                blocks[pair, half, 1 - half] = np.sin(angle)
    return blocks / np.sqrt(count)


def stacked_tables(table):
    high, low = split_bf16(table.astype(np.float32))
    return np.concatenate([high, low], axis=1)


def x_tables():
    blocks = pair_blocks(2048)
    q = blocks.reshape(PAIRS, 2, 2, 128, 16, 8)
    rows = np.transpose(q, (0, 4, 1, 5, 2, 3))
    return stacked_tables(rows.reshape(PAIRS, 256, 256))


def y_tables():
    blocks = pair_blocks(512)
    v = blocks.reshape(PAIRS, 2, 2, 32, 8, 4)
    full = np.einsum("pabrdv,jk->pdvjabrk", v, np.eye(4))
    return stacked_tables(full.reshape(PAIRS, 256, 256))


def z_table():
    src, zc, j = np.meshgrid(np.arange(8), np.arange(8), np.arange(4), indexing="ij")
    z = (32 * src + 8 * j + zc).reshape(-1)
    k = np.arange(256)
    angle = 2 * np.pi * ((z[:, None] * k[None, :]) % 256) / 256
    table = ((np.cos(angle) + np.sin(angle)) / 16.0).astype(np.float32)
    high, low = split_bf16(table)
    return np.concatenate([high, low], axis=1)


def small_hartley(v):
    n = len(v)
    if n == 1:
        return v
    half = n // 2
    even = small_hartley(v[0::2])
    odd = small_hartley(v[1::2])
    out = [None] * n
    for k in range(half):
        c = float(np.cos(2 * np.pi * k / n))
        s = float(np.sin(2 * np.pi * k / n))
        back = odd[-k % half]
        if k == 0:
            turned = odd[0]
        elif 4 * k == n:
            turned = back
        elif 8 * k == n:
            turned = (odd[k] + back) * c
        elif 8 * k == 3 * n:
            turned = (back - odd[k]) * s
        else:
            turned = odd[k] * c + back * s
        out[k] = even[k] + turned
        out[k + half] = even[k] - turned
    return out


NT = (((1,), (1,)), ((), ()))
TN = (((0,), (0,)), ((), ()))


def radix_step(load, high_ref, low_ref):
    def rows(t, carry):
        zz, g = t // 8, t % 8
        parts = small_hartley(load(zz, g))
        at = pl.ds(pl.multiple_of(zz * 128 + g * 16, 16), 16)
        for pair in range(PAIRS):
            for half, p in enumerate(partner(pair)):
                value = parts[p]
                high = value.astype(jnp.bfloat16)
                low = (value - high.astype(jnp.float32)).astype(jnp.bfloat16)
                lanes = slice(half * LANES, (half + 1) * LANES)
                high_ref[pair, at, lanes] = high
                low_ref[pair, at, lanes] = low
        return carry

    lax.fori_loop(0, 16, rows, 0)


def matmul_step(table_ref, high_ref, low_ref, store):
    def some(i, carry):
        for j in range(UNROLL):
            pair = i * UNROLL + j
            table = table_ref[pair]
            both = lax.dot_general(table, high_ref[pair], NT, preferred_element_type=jnp.float32)
            rest = lax.dot_general(table[:256], low_ref[pair], NT, preferred_element_type=jnp.float32)
            store(pair, both[:256] + both[256:] + rest)
        return carry

    lax.fori_loop(0, PAIRS // UNROLL, some, 0)


def transform_kernel(
    x_hbm, wx_hbm, wy_hbm, h_hbm, sx_hbm, sy_hbm, sz_hbm, l_hbm, r_hbm, o_ref,
    x_ref, wx_ref, wy_ref, h_ref, sx_ref, sy_ref, sz_ref, xo_ref, lb_ref, zb_ref, zt_ref, high_ref, low_ref,
    stage_ref, base_ref, turn_ref,
    load_sem, table_sem, fetch_sem, zb_sem, zt_sem,
    l_send, l_recv, l_own, r_send, r_recv, r_own, tail_send, tail_recv,
):
    left = lax.axis_index("left")
    right = lax.axis_index("right")

    def left_to(o):
        m = 16 - o
        dx, dy, dc = m // 8, m // 2 % 4, m % 2
        return lax.rem(left // 4 + dy, 4) * 4 + lax.rem(left // 2 + dx, 2) * 2 + lax.rem(left + dc, 2)

    def right_to(o):
        m = 8 - o
        dx, dz = m // 4, m % 4
        return lax.rem(right // 2 + dz, 4) * 2 + lax.rem(right + dx, 2)

    def each(first, last, action):
        def one(i, carry):
            action(i)
            return carry

        lax.fori_loop(first, last, one, 0)

    def x_load(f, g, a):
        rows = pl.ds(pl.multiple_of(g * LANES, LANES), LANES)
        lanes = pl.ds(pl.multiple_of(a * LANES, LANES), LANES)
        return pltpu.make_async_copy(x_hbm.at[f, rows, lanes], x_ref.at[a, rows], load_sem.at[g, a])

    def x_start(f):
        each(0, 8, lambda g: each(0, RADIX, lambda a: x_load(f, g, a).start()))

    wx_load = pltpu.make_async_copy(wx_hbm, wx_ref, table_sem.at[0])
    other_loads = [
        pltpu.make_async_copy(source, target, table_sem.at[1 + i])
        for i, (source, target) in enumerate(
            ((wy_hbm, wy_ref), (h_hbm, h_ref), (sx_hbm, sx_ref), (sy_hbm, sy_ref), (sz_hbm, sz_ref))
        )
    ]

    x_start(0)
    wx_load.start()

    barrier = pltpu.get_barrier_semaphore()

    def greet(device):
        pl.semaphore_signal(barrier, inc=1, device_id=device, device_id_type=MESH)

    each(1, 16, lambda o: greet((left_to(o), right)))
    each(1, 8, lambda o: greet((left, right_to(o))))
    pl.semaphore_wait(barrier, 22)
    for load in other_loads:
        load.start()

    def l_copy(c, o):
        to = left_to(o)
        return pltpu.make_async_remote_copy(
            src_ref=xo_ref.at[c, to],
            dst_ref=l_hbm.at[c, left],
            send_sem=l_send.at[c, o],
            recv_sem=l_recv.at[c, o],
            device_id=(to, right),
            device_id_type=MESH,
        )

    def l_keep(c):
        return pltpu.make_async_copy(xo_ref.at[c, left], l_hbm.at[c, left], l_own.at[c])

    yo_ref = xo_ref.reshape(CHUNKS, 8, 4, PAIRS, 16, LANES)

    def r_rows(c):
        return pl.ds(pl.multiple_of((c % 4) * 16, 16), 16)

    def r_copy(c, o):
        to = right_to(o)
        return pltpu.make_async_remote_copy(
            src_ref=yo_ref.at[c, to],
            dst_ref=r_hbm.at[right, c // 4, :, :, r_rows(c)],
            send_sem=r_send.at[c, o],
            recv_sem=r_recv.at[c, o],
            device_id=(left, to),
            device_id_type=MESH,
        )

    def r_keep(c):
        return pltpu.make_async_copy(
            yo_ref.at[c, right], r_hbm.at[right, c // 4, :, :, r_rows(c)], r_own.at[c]
        )

    def tail_copy(v, o):
        to = right_to(o)
        return pltpu.make_async_remote_copy(
            src_ref=yo_ref.at[CHUNKS - 1, to, v],
            dst_ref=zt_ref.at[1, right, v],
            send_sem=tail_send.at[v, o],
            recv_sem=tail_recv.at[v, o],
            device_id=(left, to),
            device_id_type=MESH,
        )

    def x_chunk(c, carry):
        @pl.when(c == 4)
        def _():
            x_start(1)

        first = (c % 4) * 2

        def load(zz, g):
            @pl.when((c % 4 == 0) & (zz == 0))
            def _():
                each(0, RADIX, lambda a: x_load(c // 4, g, a).wait())

            rows = pl.ds(g * LANES + first + zz, 16, stride=8)
            return [x_ref[a, rows, :] for a in range(RADIX)]

        def store(pair, value):
            at = pl.ds(pl.multiple_of(pair * 16, 16), 16)
            for zz in range(2):
                xo_ref[c, :, zz, at, :] = value[:, zz * LANES : (zz + 1) * LANES].reshape(16, 16, LANES)

        radix_step(load, high_ref, low_ref)

        @pl.when(c == 0)
        def _():
            wx_load.wait()

        matmul_step(wx_ref, high_ref, low_ref, store)
        each(1, 16, lambda o: l_copy(c, o).start())
        l_keep(c).start()
        return carry

    lax.fori_loop(0, CHUNKS, x_chunk, 0)
    for load in other_loads:
        load.wait()

    turn_ref[...] = jnp.transpose(jnp.broadcast_to(sx_ref[pl.ds(left, 1), :], (LANES, LANES)))
    for pair in range(PAIRS):
        for half, p in enumerate(partner(pair)):
            at = pair * 16 + half * 8
            column = turn_ref[pl.ds(p, 8, stride=16), :]
            for lane in range(2):
                lanes = slice(lane * LANES, (lane + 1) * LANES)
                base_ref[at : at + 8, lanes] = column + sz_ref[:, lanes]

    def y_chunk(c, carry):
        l_keep(c).wait()
        each(1, 16, lambda o: l_copy(c, o).wait_recv())
        fetch = pltpu.make_async_copy(l_hbm.at[c], lb_ref, fetch_sem)
        fetch.start()
        each(1, 16, lambda o: l_copy(c, o).wait_send())
        fetch.wait()

        def load(zz, g):
            rows = pl.ds(pl.multiple_of(g * 16, 16), 16)
            return [lb_ref[s, zz, rows, :] for s in range(RADIX)]

        def store(pair, value):
            for zz in range(2):
                yo_ref[c, :, :, pair, zz * 8 : (zz + 1) * 8, :] = value[:, zz * LANES : (zz + 1) * LANES].reshape(
                    8, 4, 8, LANES
                )

        radix_step(load, high_ref, low_ref)
        matmul_step(wy_ref, high_ref, low_ref, store)

        @pl.when(c < CHUNKS - 1)
        def _():
            each(1, 8, lambda o: r_copy(c, o).start())
            r_keep(c).start()

        return carry

    lax.fori_loop(0, CHUNKS, y_chunk, 0)
    each(0, 4, lambda v: each(1, 8, lambda o: tail_copy(v, o).start()))
    zt_ref[1, right] = yo_ref[CHUNKS - 1, right]

    def r_arrived(c):
        each(1, 8, lambda o: r_copy(c, o).wait_recv())
        r_keep(c).wait()

    def zb_fetch(unit):
        slot = unit % 2
        return pltpu.make_async_copy(
            r_hbm.at[:, unit // 4, unit % 4, :, 0:48], zb_ref.at[slot], zb_sem.at[slot]
        )

    zt_fetch = pltpu.make_async_copy(r_hbm.at[:, 0, :, :, 48:64], zt_ref.at[0], zt_sem)

    def z_unit(unit):
        f, v, slot = unit // 4, unit % 4, unit % 2
        for pair in range(PAIRS):
            for half, u in enumerate(partner(pair)):
                rows = []
                for src in range(8):
                    rows.append(zb_ref[slot, src, pair, pl.ds(half, 24, stride=2), :])
                    rows.append(zt_ref[f, src, v, pair, pl.ds(half, 8, stride=2), :])
                value = jnp.concatenate(rows, axis=0)
                high = value.astype(jnp.bfloat16)
                low = (value - high.astype(jnp.float32)).astype(jnp.bfloat16)
                lanes = slice(u % 2 * LANES, (u % 2 + 1) * LANES)
                high_ref[u // 2, :, lanes] = high
                low_ref[u // 2, :, lanes] = low

        def some(t, carry):
            both = lax.dot_general(high_ref[t], h_ref[...], TN, preferred_element_type=jnp.float32)
            rest = lax.dot_general(low_ref[t], h_ref[:, :256], TN, preferred_element_type=jnp.float32)
            acc = both[:, :256] + both[:, 256:] + rest
            for i in range(2):
                u = t * 2 + i
                scale = lax.rsqrt(base_ref[...] + sy_ref[right * 64 + v * 16 + u])
                value = acc[i * LANES : (i + 1) * LANES] * scale
                for lane in range(2):
                    at = pl.ds(pl.multiple_of(u * PITCH, 8), LANES)
                    stage_ref[lane, at, :] = value[:, lane * LANES : (lane + 1) * LANES]
            return carry

        lax.fori_loop(0, PAIRS, some, 0)

        def out_rows(q, carry):
            for pair in range(PAIRS):
                for half, p in enumerate(partner(pair)):
                    for part in range(2):
                        for lane in range(2):
                            at = part * 8 * PITCH + pair * 16 + half * 8
                            o_ref[f, q * 16 + p, v * 2 + part, lane] = stage_ref[lane, pl.ds(at + q, 8, stride=PITCH), :]
            return carry

        lax.fori_loop(0, 8, out_rows, 0)

    each(0, 4, r_arrived)
    zt_fetch.start()
    zb_fetch(0).start()
    zt_fetch.wait()

    def units(unit, carry):
        zb_fetch(unit).wait()

        @pl.when(unit == 3)
        def _():
            each(4, CHUNKS - 1, r_arrived)

        @pl.when(unit < 7)
        def _():
            zb_fetch(unit + 1).start()

        @pl.when(unit >= 4)
        def _():
            each(1, 8, lambda o: tail_copy(unit - 4, o).wait_recv())

        z_unit(unit)
        return carry

    lax.fori_loop(0, 8, units, 0)
    each(0, CHUNKS - 1, lambda c: each(1, 8, lambda o: r_copy(c, o).wait_send()))
    each(0, 4, lambda v: each(1, 8, lambda o: tail_copy(v, o).wait_send()))


def transform(x, sx, sy, sz):
    f32 = jnp.float32
    bf16 = jnp.bfloat16
    dma = pltpu.SemaphoreType.DMA
    hbm = pl.BlockSpec(memory_space=pltpu.HBM)
    _, _, out = pl.pallas_call(
        transform_kernel,
        out_shape=(
            jax.ShapeDtypeStruct((CHUNKS, 16, 2, 128, LANES), f32),
            jax.ShapeDtypeStruct((8, 2, 4, PAIRS, 64, LANES), f32),
            pltpu.VMEM((2, 128, 8, 2, 8, LANES), f32),
        ),
        in_specs=[hbm] * 7,
        out_specs=(hbm, hbm, pl.BlockSpec(memory_space=pltpu.VMEM)),
        scratch_shapes=[
            pltpu.VMEM((RADIX, 1024, LANES), f32),
            pltpu.VMEM((PAIRS, 512, 256), bf16),
            pltpu.VMEM((PAIRS, 512, 256), bf16),
            pltpu.VMEM((256, 512), bf16),
            pltpu.VMEM((16, LANES), f32),
            pltpu.SMEM((512,), f32),
            pltpu.VMEM((1, 256), f32),
            pltpu.VMEM((CHUNKS, 16, 2, 128, LANES), f32),
            pltpu.VMEM((16, 2, 128, LANES), f32),
            pltpu.VMEM((2, 8, PAIRS, 48, LANES), f32),
            pltpu.VMEM((2, 8, 4, PAIRS, 16, LANES), f32),
            pltpu.VMEM((PAIRS, 256, 256), bf16),
            pltpu.VMEM((PAIRS, 256, 256), bf16),
            pltpu.VMEM((2, 16 * PITCH, LANES), f32),
            pltpu.VMEM((128, 256), f32),
            pltpu.VMEM((LANES, LANES), f32),
            dma((8, RADIX)),
            dma((6,)),
            dma,
            dma((2,)),
            dma,
            dma((CHUNKS, 16)),
            dma((CHUNKS, 16)),
            dma((CHUNKS,)),
            dma((CHUNKS, 8)),
            dma((CHUNKS, 8)),
            dma((CHUNKS,)),
            dma((4, 8)),
            dma((4, 8)),
        ],
        compiler_params=pltpu.CompilerParams(
            collective_id=0, has_side_effects=True, vmem_limit_bytes=VMEM_BYTES
        ),
        name="transform",
    )(x, x_tables(), y_tables(), z_table(), sx, sy, sz)
    return jnp.transpose(out, (0, 1, 2, 4, 3, 5)).reshape(2, 128, 64, 256)


def local(tracer, symbol_x, symbol_y, symbol_z):
    x = jnp.transpose(tracer, (0, 2, 3, 1)).reshape(2, 1024, 2048)
    return transform(x, symbol_x.reshape(16, LANES), symbol_y, symbol_z.reshape(1, 256))


def solution(mesh):
    in_specs = (P(None, None, "left", "right"), P(), P(), P())
    out_specs = P(None, "left", "right", None)
    return jax.shard_map(local, mesh=mesh, in_specs=in_specs, out_specs=out_specs, check_vma=False)
```

time: 425 us -> 392 us (0.922)
  Pallas kernels: 419 us -> 386 us
    pallas_call x2 -> x1, Pallas kernels: 419 us -> 386 us  [transform(): pl.pallas_call(transform_kernel, out_shape=(jax.ShapeDtypeStruct((CHUNKS,...]
    unnamed x0 -> x1, local copies, waits for them, and re-layouts: none -> 6.16 us
where the time goes in v2:
time: 392 us
  Pallas kernels  386 us (98%)
  local copies, waits for them, and re-layouts  6.16 us (2%)
    pallas_call x1, Pallas kernels, transform(): pl.pallas_call(transform_kernel, out_shape=(jax.ShapeDtypeStruct((CHUNKS,...  386 us

profile of v2, /device:TPU:0, one launch (start us, length us, event | category | flops | bytes accessed | tf_op | source)
XLA Modules:
  0.0 392.1 jit_solution(3447373316711475582)
XLA Ops:
  0.0 385.9 %transform.1 = (f32[8,16,2,128,128]{4,3,2,1,0:T(8,128)}, f32[8,2,4,8,64,128]{5,4,3,2,1,0:T(8,128)}, f32[2,128,8,2,8,128]{5,4,3,2,1,0:T(8,128)S(1)}) custom-call(f32[2,1024,2048]{2,1,0:T(8,128)} %bitcast.9, bf16[8,512,256]{2,1,0:T(8,128)(2,1)} %constant.6.clone.wx_hbm, bf16[8,512,256]{2,1,0:T(8,128)(2,1)} %constant.7.clone.wy_hbm, ...), custom_call_target="tpu_custom_call" | custom-call | tf_op jit(solution)/shard_map/transform/pallas_call | solution.py:402
  385.9 6.2 %copy.9 = f32[2,128,64,256]{3,2,1,0:T(8,128)} copy(f32[2,128,64,256]{3,2,1,0:T(8,128)S(1)} %bitcast.8) | data formatting | bytes 33554432

commit v3 on v2

--- a/solution.py
+++ b/solution.py
@@ -11,7 +11,7 @@
 PAIRS = 8
 LANES = 128
 CHUNKS = 8
-VMEM_BYTES = 46 * 2**20
+VMEM_BYTES = 44 * 2**20
 PITCH = 136
 UNROLL = 2
 
@@ -134,11 +134,47 @@
     lax.fori_loop(0, PAIRS // UNROLL, some, 0)
 
 
+def z_core(rows_of, scale_of, write, h_ref, high_ref, low_ref, stage_ref):
+    for pair in range(PAIRS):
+        for half, u in enumerate(partner(pair)):
+            value = jnp.concatenate(rows_of(pair, half), axis=0)
+            high = value.astype(jnp.bfloat16)
+            low = (value - high.astype(jnp.float32)).astype(jnp.bfloat16)
+            lanes = slice(u % 2 * LANES, (u % 2 + 1) * LANES)
+            high_ref[u // 2, :, lanes] = high
+            low_ref[u // 2, :, lanes] = low
+
+    def some(t, carry):
+        both = lax.dot_general(high_ref[t], h_ref[...], TN, preferred_element_type=jnp.float32)
+        rest = lax.dot_general(low_ref[t], h_ref[:, :256], TN, preferred_element_type=jnp.float32)
+        acc = both[:, :256] + both[:, 256:] + rest
+        for i in range(2):
+            u = t * 2 + i
+            value = acc[i * LANES : (i + 1) * LANES] * scale_of(u)
+            for lane in range(2):
+                at = pl.ds(pl.multiple_of(u * PITCH, 8), LANES)
+                stage_ref[lane, at, :] = value[:, lane * LANES : (lane + 1) * LANES]
+        return carry
+
+    lax.fori_loop(0, PAIRS, some, 0)
+
+    def out_rows(q, carry):
+        for pair in range(PAIRS):
+            for half, p in enumerate(partner(pair)):
+                for part in range(2):
+                    for lane in range(2):
+                        at = part * 8 * PITCH + pair * 16 + half * 8
+                        write(q * 16 + p, part, lane, stage_ref[lane, pl.ds(at + q, 8, stride=PITCH), :])
+        return carry
+
+    lax.fori_loop(0, 8, out_rows, 0)
+
+
 def transform_kernel(
-    x_hbm, wx_hbm, wy_hbm, h_hbm, sx_hbm, sy_hbm, sz_hbm, l_hbm, r_hbm, o_ref,
-    x_ref, wx_ref, wy_ref, h_ref, sx_ref, sy_ref, sz_ref, xo_ref, lb_ref, zb_ref, zt_ref, high_ref, low_ref,
-    stage_ref, base_ref, turn_ref,
-    load_sem, table_sem, fetch_sem, zb_sem, zt_sem,
+    x_hbm, wx_hbm, wy_hbm, h_hbm, sx_hbm, sy_hbm, sz_hbm, l_hbm, r_hbm, o_ref, last_ref, base_ref, level_ref, h_ref,
+    x_ref, wx_ref, wy_ref, sx_ref, sy_ref, sz_ref, xo_ref, lb_ref, zb_ref, zt_ref, high_ref, low_ref,
+    stage_ref, turn_ref,
+    load_sem, table_sem, fetch_sem, zb_sem, zt_sem, last_sem,
     l_send, l_recv, l_own, r_send, r_recv, r_own, tail_send, tail_recv,
 ):
     left = lax.axis_index("left")
@@ -161,13 +197,13 @@
 
         lax.fori_loop(first, last, one, 0)
 
-    def x_load(f, g, a):
-        rows = pl.ds(pl.multiple_of(g * LANES, LANES), LANES)
+    def x_load(c, a):
+        two = pl.ds(c % 4 * 2, 2)
         lanes = pl.ds(pl.multiple_of(a * LANES, LANES), LANES)
-        return pltpu.make_async_copy(x_hbm.at[f, rows, lanes], x_ref.at[a, rows], load_sem.at[g, a])
-
-    def x_start(f):
-        each(0, 8, lambda g: each(0, RADIX, lambda a: x_load(f, g, a).start()))
+        return pltpu.make_async_copy(x_hbm.at[c // 4, :, two, lanes], x_tiles.at[a, :, two], load_sem.at[c, a])
+
+    def x_start(c):
+        each(0, RADIX, lambda a: x_load(c, a).start())
 
     wx_load = pltpu.make_async_copy(wx_hbm, wx_ref, table_sem.at[0])
     other_loads = [
@@ -177,8 +213,12 @@
         )
     ]
 
+    x_tiles = x_ref.reshape(RADIX, LANES, 8, LANES)
     x_start(0)
     wx_load.start()
+    each(1, 4, x_start)
+    for load in other_loads:
+        load.start()
 
     barrier = pltpu.get_barrier_semaphore()
 
@@ -187,9 +227,6 @@
 
     each(1, 16, lambda o: greet((left_to(o), right)))
     each(1, 8, lambda o: greet((left, right_to(o))))
-    pl.semaphore_wait(barrier, 22)
-    for load in other_loads:
-        load.start()
 
     def l_copy(c, o):
         to = left_to(o)
@@ -237,18 +274,30 @@
             device_id_type=MESH,
         )
 
-    def x_chunk(c, carry):
+    def last_copy(o):
+        to = right_to(o)
+        return pltpu.make_async_remote_copy(
+            src_ref=yo_ref.at[CHUNKS - 1, to, 3],
+            dst_ref=last_ref.at[right, :, 48:64],
+            send_sem=tail_send.at[3, o],
+            recv_sem=tail_recv.at[3, o],
+            device_id=(left, to),
+            device_id_type=MESH,
+        )
+
+    def x_chunk(c, first_time=False):
+        @pl.when(c == 3)
+        def _():
+            x_start(4)
+
         @pl.when(c == 4)
         def _():
-            x_start(1)
-
+            each(5, 8, x_start)
+
+        each(0, RADIX, lambda a: x_load(c, a).wait())
         first = (c % 4) * 2
 
         def load(zz, g):
-            @pl.when((c % 4 == 0) & (zz == 0))
-            def _():
-                each(0, RADIX, lambda a: x_load(c // 4, g, a).wait())
-
             rows = pl.ds(g * LANES + first + zz, 16, stride=8)
             return [x_ref[a, rows, :] for a in range(RADIX)]
 
@@ -259,29 +308,16 @@
 
         radix_step(load, high_ref, low_ref)
 
-        @pl.when(c == 0)
-        def _():
+        if first_time:
             wx_load.wait()
 
         matmul_step(wx_ref, high_ref, low_ref, store)
+
+    def x_send(c):
         each(1, 16, lambda o: l_copy(c, o).start())
         l_keep(c).start()
-        return carry
-
-    lax.fori_loop(0, CHUNKS, x_chunk, 0)
-    for load in other_loads:
-        load.wait()
-
-    turn_ref[...] = jnp.transpose(jnp.broadcast_to(sx_ref[pl.ds(left, 1), :], (LANES, LANES)))
-    for pair in range(PAIRS):
-        for half, p in enumerate(partner(pair)):
-            at = pair * 16 + half * 8
-            column = turn_ref[pl.ds(p, 8, stride=16), :]
-            for lane in range(2):
-                lanes = slice(lane * LANES, (lane + 1) * LANES)
-                base_ref[at : at + 8, lanes] = column + sz_ref[:, lanes]
-
-    def y_chunk(c, carry):
+
+    def y_chunk(c):
         l_keep(c).wait()
         each(1, 16, lambda o: l_copy(c, o).wait_recv())
         fetch = pltpu.make_async_copy(l_hbm.at[c], lb_ref, fetch_sem)
@@ -307,11 +343,17 @@
             each(1, 8, lambda o: r_copy(c, o).start())
             r_keep(c).start()
 
-        return carry
-
-    lax.fori_loop(0, CHUNKS, y_chunk, 0)
-    each(0, 4, lambda v: each(1, 8, lambda o: tail_copy(v, o).start()))
-    zt_ref[1, right] = yo_ref[CHUNKS - 1, right]
+    def prepare_scale():
+        turn_ref[...] = jnp.transpose(jnp.broadcast_to(sx_ref[pl.ds(left, 1), :], (LANES, LANES)))
+        for pair in range(PAIRS):
+            for half, p in enumerate(partner(pair)):
+                at = pair * 16 + half * 8
+                column = turn_ref[pl.ds(p, 8, stride=16), :]
+                for lane in range(2):
+                    lanes = slice(lane * LANES, (lane + 1) * LANES)
+                    base_ref[at : at + 8, lanes] = column + sz_ref[:, lanes]
+        for u in range(16):
+            level_ref[u * 8 : u * 8 + 8, :] = jnp.full((8, LANES), sy_ref[right * 64 + 48 + u])
 
     def r_arrived(c):
         each(1, 8, lambda o: r_copy(c, o).wait_recv())
@@ -327,58 +369,52 @@
 
     def z_unit(unit):
         f, v, slot = unit // 4, unit % 4, unit % 2
-        for pair in range(PAIRS):
-            for half, u in enumerate(partner(pair)):
-                rows = []
-                for src in range(8):
-                    rows.append(zb_ref[slot, src, pair, pl.ds(half, 24, stride=2), :])
-                    rows.append(zt_ref[f, src, v, pair, pl.ds(half, 8, stride=2), :])
-                value = jnp.concatenate(rows, axis=0)
-                high = value.astype(jnp.bfloat16)
-                low = (value - high.astype(jnp.float32)).astype(jnp.bfloat16)
-                lanes = slice(u % 2 * LANES, (u % 2 + 1) * LANES)
-                high_ref[u // 2, :, lanes] = high
-                low_ref[u // 2, :, lanes] = low
-
-        def some(t, carry):
-            both = lax.dot_general(high_ref[t], h_ref[...], TN, preferred_element_type=jnp.float32)
-            rest = lax.dot_general(low_ref[t], h_ref[:, :256], TN, preferred_element_type=jnp.float32)
-            acc = both[:, :256] + both[:, 256:] + rest
-            for i in range(2):
-                u = t * 2 + i
-                scale = lax.rsqrt(base_ref[...] + sy_ref[right * 64 + v * 16 + u])
-                value = acc[i * LANES : (i + 1) * LANES] * scale
-                for lane in range(2):
-                    at = pl.ds(pl.multiple_of(u * PITCH, 8), LANES)
-                    stage_ref[lane, at, :] = value[:, lane * LANES : (lane + 1) * LANES]
-            return carry
-
-        lax.fori_loop(0, PAIRS, some, 0)
-
-        def out_rows(q, carry):
-            for pair in range(PAIRS):
-                for half, p in enumerate(partner(pair)):
-                    for part in range(2):
-                        for lane in range(2):
-                            at = part * 8 * PITCH + pair * 16 + half * 8
-                            o_ref[f, q * 16 + p, v * 2 + part, lane] = stage_ref[lane, pl.ds(at + q, 8, stride=PITCH), :]
-            return carry
-
-        lax.fori_loop(0, 8, out_rows, 0)
-
-    each(0, 4, r_arrived)
-    zt_fetch.start()
-    zb_fetch(0).start()
-    zt_fetch.wait()
-
-    def units(unit, carry):
+
+        def rows_of(pair, half):
+            rows = []
+            for src in range(8):
+                rows.append(zb_ref[slot, src, pair, pl.ds(half, 24, stride=2), :])
+                rows.append(zt_ref[f, src, v, pair, pl.ds(half, 8, stride=2), :])
+            return rows
+
+        def scale_of(u):
+            return lax.rsqrt(base_ref[...] + sy_ref[right * 64 + v * 16 + u])
+
+        def write(kx, part, lane, value):
+            o_ref[f, kx, v * 2 + part, lane] = value
+
+        z_core(rows_of, scale_of, write, h_ref, high_ref, low_ref, stage_ref)
+
+    last_fetch = pltpu.make_async_copy(r_hbm.at[:, 1, 3, :, 0:48], last_ref.at[:, :, 0:48], last_sem)
+
+    def y_step(c):
+        y_chunk(c)
+
+        @pl.when(c == CHUNKS - 1)
+        def _():
+            each(0, 3, lambda v: each(1, 8, lambda o: tail_copy(v, o).start()))
+            each(1, 8, lambda o: last_copy(o).start())
+            zt_ref[1, right, 0:3] = yo_ref[CHUNKS - 1, right, 0:3]
+            last_ref[right, :, 48:64] = yo_ref[CHUNKS - 1, right, 3]
+
+    def z_step(unit):
+        @pl.when(unit == 0)
+        def _():
+            prepare_scale()
+            each(0, 4, r_arrived)
+            zt_fetch.start()
+            zb_fetch(0).start()
+            zt_fetch.wait()
+
+        @pl.when(unit == 4)
+        def _():
+            each(4, CHUNKS - 1, r_arrived)
+            zb_fetch(4).start()
+            last_fetch.start()
+
         zb_fetch(unit).wait()
 
-        @pl.when(unit == 3)
-        def _():
-            each(4, CHUNKS - 1, r_arrived)
-
-        @pl.when(unit < 7)
+        @pl.when((unit % 4 < 3) & (unit < 6))
         def _():
             zb_fetch(unit + 1).start()
 
@@ -387,11 +423,36 @@
             each(1, 8, lambda o: tail_copy(unit - 4, o).wait_recv())
 
         z_unit(unit)
-        return carry
-
-    lax.fori_loop(0, 8, units, 0)
+
+    def step(i):
+        @pl.when(((i >= 2) & (i < 9)) | (i == 13))
+        def _():
+            y_step(i - 2 - 4 * (i // 13))
+
+        @pl.when((i >= 1) & (i < CHUNKS))
+        def _():
+            x_chunk(i)
+
+        @pl.when(i < CHUNKS)
+        def _():
+            x_send(i)
+
+        @pl.when(i == 1)
+        def _():
+            for load in other_loads:
+                load.wait()
+
+        @pl.when(((i >= 9) & (i < 13)) | (i >= 14))
+        def _():
+            z_step(i - 9 - i // 13)
+
+    x_chunk(0, True)
+    pl.semaphore_wait(barrier, 22)
+    each(0, 17, step)
+    last_fetch.wait()
+    each(1, 8, lambda o: last_copy(o).wait())
     each(0, CHUNKS - 1, lambda c: each(1, 8, lambda o: r_copy(c, o).wait_send()))
-    each(0, 4, lambda v: each(1, 8, lambda o: tail_copy(v, o).wait_send()))
+    each(0, 3, lambda v: each(1, 8, lambda o: tail_copy(v, o).wait_send()))
 
 
 def transform(x, sx, sy, sz):
@@ -399,20 +460,23 @@
     bf16 = jnp.bfloat16
     dma = pltpu.SemaphoreType.DMA
     hbm = pl.BlockSpec(memory_space=pltpu.HBM)
-    _, _, out = pl.pallas_call(
+    _, _, out, rest, base, level, table = pl.pallas_call(
         transform_kernel,
         out_shape=(
             jax.ShapeDtypeStruct((CHUNKS, 16, 2, 128, LANES), f32),
             jax.ShapeDtypeStruct((8, 2, 4, PAIRS, 64, LANES), f32),
             pltpu.VMEM((2, 128, 8, 2, 8, LANES), f32),
+            pltpu.VMEM((8, PAIRS, 64, LANES), f32),
+            pltpu.VMEM((128, 256), f32),
+            pltpu.VMEM((128, LANES), f32),
+            pltpu.VMEM((256, 512), bf16),
         ),
         in_specs=[hbm] * 7,
-        out_specs=(hbm, hbm, pl.BlockSpec(memory_space=pltpu.VMEM)),
+        out_specs=(hbm, hbm) + (pl.BlockSpec(memory_space=pltpu.VMEM),) * 5,
         scratch_shapes=[
             pltpu.VMEM((RADIX, 1024, LANES), f32),
             pltpu.VMEM((PAIRS, 512, 256), bf16),
             pltpu.VMEM((PAIRS, 512, 256), bf16),
-            pltpu.VMEM((256, 512), bf16),
             pltpu.VMEM((16, LANES), f32),
             pltpu.SMEM((512,), f32),
             pltpu.VMEM((1, 256), f32),
@@ -423,12 +487,12 @@
             pltpu.VMEM((PAIRS, 256, 256), bf16),
             pltpu.VMEM((PAIRS, 256, 256), bf16),
             pltpu.VMEM((2, 16 * PITCH, LANES), f32),
-            pltpu.VMEM((128, 256), f32),
             pltpu.VMEM((LANES, LANES), f32),
-            dma((8, RADIX)),
+            dma((CHUNKS, RADIX)),
             dma((6,)),
             dma,
             dma((2,)),
+            dma,
             dma,
             dma((CHUNKS, 16)),
             dma((CHUNKS, 16)),
@@ -444,11 +508,58 @@
         ),
         name="transform",
     )(x, x_tables(), y_tables(), z_table(), sx, sy, sz)
+    return finish(out, rest, base, level, table)
+
+
+def finish_kernel(
+    done_ref, last_ref, base_ref, level_ref, h_ref, o_hbm, high_ref, low_ref, stage_ref, out_ref, sem
+):
+    first = pltpu.make_async_copy(done_ref.at[0], o_hbm.at[0], sem.at[0])
+    second = pltpu.make_async_copy(done_ref.at[1, :, 0:6], o_hbm.at[1, :, 0:6], sem.at[1])
+    third = pltpu.make_async_copy(out_ref, o_hbm.at[1, :, 6:8], sem.at[2])
+    first.start()
+    second.start()
+
+    def rows_of(pair, half):
+        return [last_ref[src, pair, pl.ds(half, 32, stride=2), :] for src in range(8)]
+
+    def scale_of(u):
+        level = level_ref[pl.ds(u * 8, 1), :]
+        return lax.rsqrt(base_ref[...] + jnp.concatenate([level, level], axis=1))
+
+    def write(kx, part, lane, value):
+        out_ref[kx, part, lane] = value
+
+    z_core(rows_of, scale_of, write, h_ref, high_ref, low_ref, stage_ref)
+    third.start()
+    first.wait()
+    second.wait()
+    third.wait()
+
+
+def finish(done, rest, base, level, table):
+    f32 = jnp.float32
+    vmem = pl.BlockSpec(memory_space=pltpu.VMEM)
+    out = pl.pallas_call(
+        finish_kernel,
+        out_shape=jax.ShapeDtypeStruct((2, 128, 8, 2, 8, LANES), f32),
+        in_specs=[vmem] * 5,
+        out_specs=pl.BlockSpec(memory_space=pltpu.HBM),
+        scratch_shapes=[
+            pltpu.VMEM((PAIRS, 256, 256), jnp.bfloat16),
+            pltpu.VMEM((PAIRS, 256, 256), jnp.bfloat16),
+            pltpu.VMEM((2, 16 * PITCH, LANES), f32),
+            pltpu.VMEM((128, 2, 2, 8, LANES), f32),
+            pltpu.SemaphoreType.DMA((3,)),
+        ],
+        compiler_params=pltpu.CompilerParams(vmem_limit_bytes=16 * 2**20),
+        name="finish",
+    )(done, rest, base, level, table)
     return jnp.transpose(out, (0, 1, 2, 4, 3, 5)).reshape(2, 128, 64, 256)
 
 
 def local(tracer, symbol_x, symbol_y, symbol_z):
-    x = jnp.transpose(tracer, (0, 2, 3, 1)).reshape(2, 1024, 2048)
+    x = jnp.transpose(tracer, (0, 2, 3, 1)).reshape(2, 128, 8, 2048)
     return transform(x, symbol_x.reshape(16, LANES), symbol_y, symbol_z.reshape(1, 256))
 
 

time: 392 us -> 384 us (0.980)
  local copies, waits for them, and re-layouts: 6.16 us -> 0 us
    pallas_call x1, Pallas kernels: 386 us -> 378 us  [transform(): pl.pallas_call(transform_kernel, out_shape=(jax.ShapeDtypeStruct((CHUNKS,...]
    unnamed x1 -> x0, local copies, waits for them, and re-layouts: 6.16 us -> none
    pallas_call x0 -> x1, Pallas kernels: none -> 6 us  [finish(): pl.pallas_call(finish_kernel, out_shape=jax.ShapeDtypeStruct((2, 128, 8,...]
where the time goes in v3:
time: 384 us
  Pallas kernels  384 us (100%)
    pallas_call x1, Pallas kernels, transform(): pl.pallas_call(transform_kernel, out_shape=(jax.ShapeDtypeStruct((CHUNKS,...  378 us

profile of v3, /device:TPU:0, one launch (start us, length us, event | category | flops | bytes accessed | tf_op | source)
XLA Modules:
  0.0 383.9 jit_solution(17037667663595992062)
XLA Ops:
  0.0 377.9 %transform.1 = (f32[8,16,2,128,128]{4,3,2,1,0:T(8,128)}, f32[8,2,4,8,64,128]{5,4,3,2,1,0:T(8,128)}, f32[2,128,8,2,8,128]{5,4,3,2,1,0:T(8,128)S(1)}, f32[8,8,64,1...) custom-call(f32[2,128,8,2048]{3,2,1,0:T(8,128)} %bitcast.8, ...), custom_call_target="tpu_custom_call" | custom-call | tf_op jit(solution)/shard_map/transform/pallas_call | solution.py:463
  377.9 6.0 %finish.1 = f32[2,128,8,2,8,128]{5,4,3,2,1,0:T(8,128)} custom-call(f32[2,128,8,2,8,128]{5,4,3,2,1,0:T(8,128)S(1)} %get-tuple-element.10.done_ref, f32[8,8,64,128]{3,2,1,0:T(8,128)S(1)} %get-tuple-element.11.last_ref, f32[128,256]{1,0:T(8,128)S(1)} %get-tuple-element.12.base_ref, f32[128,128]{1,0:T(8,128)S(1)} %get-tuple-element.13.level_ref, ...), custom_call_target="tpu_custom_call" | custom-call | tf_op jit(solution)/shard_map/finish/pallas_call | solution.py:543
